TPU v7x, 32 devices: a whole 2x2x4 slice. The times are simulated.
32 devices in a mesh: batch: 4 (over y, x), ctx: 8 (over z, core).
Axes of the slice: x: 2, y: 2, z: 4, core: 2. Of those that a mesh axis runs over, the one named last changes fastest.
Arguments:
- asked_for: bfloat16 [4, 1024, 64, 64], P('batch', 'ctx'), may hold values from -6 to 6
- offered: bfloat16 [4, 1024, 64, 64], P('batch', 'ctx'), may hold values from -6 to 6
- contents: bfloat16 [4, 1024, 64, 64], P('batch', 'ctx'), may hold values from -6 to 6
- out_weight: bfloat16 [4096, 4096], P('batch'), may hold values from -0.09375 to 0.09375
Outputs:
- layer_out: bfloat16 [4, 1024, 4096], P('batch', 'ctx')
All inputs are finite; a program needn't handle non-finite values.
Results may differ from a plain program's by a relative error of at most 0.006.
Values may be sent and summed in bfloat16 or wider, within the bound.
A program may use at most 128 MiB of HBM per device.

v0:
```python
import jax
import jax.numpy as jnp
from jax import lax
from jax.sharding import PartitionSpec as P


def to_features(values):
    wide = values.astype(jnp.float32)
    return jax.nn.softplus(wide).astype(jnp.bfloat16)


def after_reading(read, count):
    result = read * count**0.5
    return result.astype(jnp.bfloat16)


def look_up(features, state, mass):
    top = jnp.einsum(
        "bthd,bhde->bthe", features, state.astype(jnp.bfloat16), preferred_element_type=jnp.float32
    )
    bottom = jnp.einsum(
        "bthd,bhd->bth", features.astype(jnp.float32), mass, precision=lax.Precision.HIGHEST
    )
    return top / (bottom + 0.001)[..., None]


def shards(asked_for, offered, contents, out_weight):
    query_feature, key_feature = (to_features(asked_for), to_features(offered))
    count = asked_for.shape[1] * lax.axis_size("ctx")
    head_query, head_key, head_value = (
        lax.all_to_all(query_feature, "ctx", split_axis=2, concat_axis=1, tiled=True),
        lax.all_to_all(key_feature, "ctx", split_axis=2, concat_axis=1, tiled=True),
        lax.all_to_all(contents, "ctx", split_axis=2, concat_axis=1, tiled=True),
    )
    state = (
        jnp.einsum("bthd,bthe->bhde", head_key, head_value, preferred_element_type=jnp.float32)
        / count
    )
    mass = jnp.sum(head_key.astype(jnp.float32), axis=1) / count
    head_read = look_up(head_query, state, mass)
    read = lax.all_to_all(head_read, "ctx", split_axis=1, concat_axis=2, tiled=True)
    mixed = after_reading(read, count)
    mixed = mixed.reshape(mixed.shape[0], mixed.shape[1], -1)
    return jnp.einsum(
        "btw,wv->btv",
        mixed,
        lax.all_gather(out_weight, "batch", axis=0, tiled=True),
        preferred_element_type=jnp.float32,
    ).astype(jnp.bfloat16)


def solution(mesh):
    in_specs = (
        P("batch", "ctx", None, None),
        P("batch", "ctx", None, None),
        P("batch", "ctx", None, None),
        P("batch", None),
    )
    out_specs = P("batch", "ctx", None)
    return jax.shard_map(shards, mesh=mesh, in_specs=in_specs, out_specs=out_specs, check_vma=False)
```

profile of v0, /device:TPU:24, one launch (start us, length us, event | category | flops | bytes accessed | tf_op | source)
XLA Modules:
  0.0 328.1 jit_solution(17906474795930241207)
XLA Ops:
  6.5 0.0 copy-start
  6.5 0.0 all-gather.2.cloned.1.call-start
  6.5 0.7 all-gather.2.cloned.1.call-update
  7.3 0.5 copy-done
  7.8 2.2 fusion.10
  10.0 0.0 copy-start.1
  10.0 5.2 %all-to-all-start.2 = ((bf16[1,128,64,64]{1,3,0,2:T(8,128)(2,1)}), bf16[1,128,64,64]{1,3,0,2:T(8,128)(2,1)S(1)}, u32[]{:S(2)}, u32[]{:S(2)}) async-start(bf16[1,128,64,64]{1,3,0,2:T(8,128)(2,1)} %fusion.10), calls=%async_computation.2 | async-start | bytes 2097152 | tf_op jit(solution)/shard_map/all_to_all | solution.py:31
  15.2 0.0 copy-done.1
  15.2 1.2 fusion.9
  16.4 22.8 %all-to-all-done.2 = bf16[1,128,64,64]{1,3,0,2:T(8,128)(2,1)S(1)} async-done(((bf16[1,128,64,64]{1,3,0,2:T(8,128)(2,1)}), bf16[1,128,64,64]{1,3,0,2:T(8,128)(2,1)S(1)}, u32[]{:S(2)}, u32[]{:S(2)}) %all-to-all-start.2) | async-done | bytes 1048608 | tf_op jit(solution)/shard_map/all_to_all | solution.py:31
  39.2 29.0 %all_to_all.54 = bf16[1,128,64,64]{1,3,0,2:T(8,128)(2,1)S(1)} all-to-all(bf16[1,128,64,64]{1,3,0,2:T(8,128)(2,1)S(1)} %fusion.9), channel_id=1, replica_groups=mesh['batch'=4,'ctx'=8] {'ctx'}, dimensions={2} | all-to-all | bytes 2097152 | tf_op jit(solution)/shard_map/all_to_all | solution.py:32
  68.2 6.0 %all-to-all-start.1 = ((bf16[1,128,64,64]{1,3,0,2:T(8,128)(2,1)}), bf16[1,128,64,64]{1,3,0,2:T(8,128)(2,1)S(1)}, u32[]{:S(2)}, u32[]{:S(2)}) async-start(bf16[1,128,64,64]{1,3,0,2:T(8,128)(2,1)} %bitcast.81), calls=%async_computation.1 | async-start | bytes 2097152 | tf_op jit(solution)/shard_map/all_to_all | solution.py:33
  74.2 1.7 copy.48
  75.9 1.5 reshape.53
  77.4 1.7 copy.50
  79.1 2.3 reshape.51
  81.4 16.8 %all-to-all-done.1 = bf16[1,128,64,64]{1,3,0,2:T(8,128)(2,1)S(1)} async-done(((bf16[1,128,64,64]{1,3,0,2:T(8,128)(2,1)}), bf16[1,128,64,64]{1,3,0,2:T(8,128)(2,1)S(1)}, u32[]{:S(2)}, u32[]{:S(2)}) %all-to-all-start.1) | async-done | bytes 1048608 | tf_op jit(solution)/shard_map/all_to_all | solution.py:33
  98.2 1.7 copy.49
  99.9 0.0 copy-start.2
  99.9 2.4 reshape.52
  102.3 1.4 convert_reduce_fusion
  103.7 0.5 fusion.15
  104.2 0.0 copy-done.2
  104.3 3.2 bitcast_divide_fusion
  107.5 3.9 %copy.35 = f32[1,1024,8,64]{3,2,0,1:T(8,128)} copy(f32[1,1024,8,64]{1,3,2,0:T(8,128)} %bitcast_divide_fusion) | data formatting | bytes 4194304 | tf_op jit(solution)/shard_map/div | solution.py:24
  111.4 5.9 %reshape.56 = f32[8,1,65536]{2,1,0:T(1,128)S(1)} reshape(f32[1024,1,8,64]{3,2,1,0:T(8,128)} %bitcast.69) | data formatting | bytes 4194304
  117.3 52.2 %all_to_all.55 = f32[8,1,65536]{2,1,0:T(1,128)} all-to-all(f32[8,1,65536]{2,1,0:T(1,128)S(1)} %reshape.56), channel_id=1, replica_groups=mesh['batch'=4,'ctx'=8] {'ctx'}, dimensions={0} | all-to-all | bytes 4194304 | tf_op jit(solution)/shard_map/all_to_all | solution.py:41
  169.6 0.5 broadcast.21
  170.1 7.2 %reduce.2 = f32[8,65536]{1,0:T(8,128)S(1)} reduce(f32[8,1,65536]{2,1,0:T(1,128)} %all_to_all.55, f32[]{:T(128)} %broadcast.21), dimensions={1}, to_apply=%all_to_all.49.reduce_sub_computation | reduce | bytes 4194308 | tf_op jit(solution)/shard_map/all_to_all | solution.py:41
  177.3 3.7 %reshape.57 = f32[1024,1,8,64]{3,2,1,0:T(8,128)} reshape(f32[8,65536]{1,0:T(8,128)S(1)} %reduce.2) | data formatting | bytes 4194304
  181.0 2.8 copy.36
  183.8 0.3 multiply_convert_fusion
  184.1 0.3 copy.41
  184.4 0.3 copy.37
  184.7 122.6 %all-gather.2.cloned.1.call-done = bf16[4096,4096]{1,0:T(8,128)(2,1)} async-done(((bf16[1024,4096]{1,0:T(8,128)(2,1)}), bf16[4096,4096]{1,0:T(8,128)(2,1)}) %all-gather.2.cloned.1.call-update) | async-done | bytes 33554448 | tf_op jit(solution)/shard_map/all_gather | solution.py:47
  307.3 14.0 %fusion = bf16[1,128,4096]{2,1,0:T(8,128)(2,1)} fusion(bf16[128,4096]{0,1:T(8,128)(2,1)S(1)} %bitcast.73, bf16[4096,4096]{1,0:T(8,128)(2,1)} %all-gather.2.cloned.1.call-done), kind=kOutput, calls=%fused_computation.3 | convolution fusion | flops 4295491584 | bytes 35651584 | tf_op jit(solution)/shard_map/btw,wv->btv/dot_general | solution.py:44
  (2 shorter events, 0.0 us)
Async XLA Ops:
  6.5 1.2 copy-start
  6.5 300.7 %all-gather.2.cloned.1.call-start = ((), (), s32[]{:S(2)}) async-start(), calls=%async_computation.4 | async-start | bytes 41943040 | tf_op jit(solution)/shard_map/all_gather | solution.py:47
  10.0 5.2 %copy-start.1 = (bf16[1,128,64,64]{1,3,2,0:T(8,128)(2,1)S(1)}, bf16[1,128,64,64]{1,3,2,0:T(8,128)(2,1)}, u32[]{:S(2)}) copy-start(bf16[1,128,64,64]{1,3,2,0:T(8,128)(2,1)} %param.5) | copy-start | bytes 3145732
  10.0 29.3 %all-to-all-start.2 = ((bf16[1,128,64,64]{1,3,0,2:T(8,128)(2,1)}), bf16[1,128,64,64]{1,3,0,2:T(8,128)(2,1)S(1)}, u32[]{:S(2)}, u32[]{:S(2)}) async-start(bf16[1,128,64,64]{1,3,0,2:T(8,128)(2,1)} %fusion.10), calls=%async_computation.2 | async-start | bytes 2097152 | tf_op jit(solution)/shard_map/all_to_all | solution.py:31
  68.2 30.0 %all-to-all-start.1 = ((bf16[1,128,64,64]{1,3,0,2:T(8,128)(2,1)}), bf16[1,128,64,64]{1,3,0,2:T(8,128)(2,1)S(1)}, u32[]{:S(2)}, u32[]{:S(2)}) async-start(bf16[1,128,64,64]{1,3,0,2:T(8,128)(2,1)} %bitcast.81), calls=%async_computation.1 | async-start | bytes 2097152 | tf_op jit(solution)/shard_map/all_to_all | solution.py:33
  99.9 4.3 %copy-start.2 = (bf16[1024,8,64]{0,2,1:T(8,128)(2,1)S(1)}, bf16[1024,8,64]{0,2,1:T(8,128)(2,1)}, u32[]{:S(2)}) copy-start(bf16[1024,8,64]{0,2,1:T(8,128)(2,1)} %reshape.51) | copy-start | bytes 3145732
Sparse Core Ops, SparseCore 0:
  9.2 298.0 all-gather.1
where the time goes:
time: 331 us; the launch traced here: 328 us
  waiting for transfers between devices  163 us (49%)
  blocking collectives  81.2 us (25%)
  local copies, waits for them, and re-layouts  29.2 us (9%)
  matrix products  17.8 us (5%)
  between operations  13.5 us (4%)
  other arithmetic  12.3 us (4%)
  starting transfers between devices  11.3 us (3%)
    all_gather x1, waiting for transfers between devices, shards(): lax.all_gather(out_weight, 'batch', axis=0, tiled=True)  123 us
    all_to_all x1, blocking collectives, shards(): lax.all_to_all(head_read, 'ctx', split_axis=1, concat_axis=2, tiled=True)  52.2 us
    all_to_all x1, blocking collectives, shards(): lax.all_to_all(key_feature, 'ctx', split_axis=2, concat_axis=1, tiled=True)  29 us
    all_to_all x1, waiting for transfers between devices, shards(): lax.all_to_all(query_feature, 'ctx', split_axis=2, concat_axis=1, tiled=T...  22.8 us
    all_to_all x1, waiting for transfers between devices, shards(): lax.all_to_all(contents, 'ctx', split_axis=2, concat_axis=1, tiled=True)  16.8 us
    dot_general x1, matrix products, shards(): jnp.einsum('btw,wv->btv', mixed, lax.all_gather(out_weight, 'batch', axis...  14 us
    unnamed x9, local copies, waits for them, and re-layouts  10.4 us
    all_to_all x1, other arithmetic, shards(): lax.all_to_all(head_read, 'ctx', split_axis=1, concat_axis=2, tiled=True)  7.22 us
  transfers between devices with their start and end apart: 3, of which 3 were waited for; matrix products, arithmetic and copies ran while one was open for 14% of the time, Pallas kernels for 0%

commit v1 on v0

v1 whole, which is shorter than its diff:
```python
import functools

import jax
import jax.numpy as jnp
from jax import lax
from jax.experimental import pallas as pl
from jax.experimental.pallas import tpu as pltpu
from jax.sharding import PartitionSpec as P

MESH = pl.DeviceIdType.MESH
LANES = 128
EXTRA = 16
CHUNK = 512


def softplus(x):
    x = x.astype(jnp.float32)
    return (jnp.maximum(x, 0.0) + jnp.log(1.0 + jnp.exp(-jnp.abs(x)))).astype(jnp.bfloat16)


def split_mass(m):
    row = lax.broadcasted_iota(jnp.int32, (EXTRA, LANES), 0)
    high = m.astype(jnp.bfloat16).astype(jnp.float32)
    return jnp.where(row == 0, high, jnp.where(row == 1, m - high, 0.0)).astype(jnp.bfloat16)


def kernel(
    nb, nc, size, q_ref, k_ref, v_ref, w_ref, o_ref,
    kt, vt, wv, qx, part, rs, own, st, mixed, out_buf, mine, in_buf,
    local_sem, q_send, q_recv, rs_send, rs_recv, ag_send, ag_recv, pr_send, pr_recv,
):
    b, c = lax.axis_index("batch"), lax.axis_index("ctx")
    rows, tokens = k_ref.shape
    pairs = rows // LANES
    ppg, ppd = pairs // nb, pairs // nc
    group = rows // nb
    total = nb * nc
    me = b * nc + c
    count = tokens * nc
    chunks = out_buf.shape[0]

    barrier = pltpu.get_barrier_semaphore()

    def greet(i, carry):
        d = lax.rem(me + i, total)
        pl.semaphore_signal(barrier, inc=1, device_id=(d // nc, lax.rem(d, nc)), device_id_type=MESH)
        return carry

    lax.fori_loop(1, total, greet, 0)
    k_copy = pltpu.make_async_copy(k_ref, kt, local_sem.at[0])
    v_copy = pltpu.make_async_copy(v_ref, vt, local_sem.at[1])
    q_copy = pltpu.make_async_copy(q_ref.at[pl.ds(b * group, group)], qx.at[0], local_sem.at[2])
    w_copy = pltpu.make_async_copy(w_ref, wv, local_sem.at[3])
    k_copy.start()
    v_copy.start()
    q_copy.start()
    w_copy.start()
    pl.semaphore_wait(barrier, total - 1)

    def q_move(k):
        to = lax.rem(b + k, nb)
        return pltpu.make_async_remote_copy(
            src_ref=q_ref.at[pl.ds(to * group, group)], dst_ref=qx.at[nb - k],
            send_sem=q_send.at[k], recv_sem=q_recv.at[nb - k],
            device_id=(to, c), device_id_type=MESH,
        )

    for k in range(1, nb):
        q_move(k).start()

    lane = lax.broadcasted_iota(jnp.int32, (size, LANES), 1) < size
    lane_x = lax.broadcasted_iota(jnp.int32, (EXTRA, LANES), 1) < size
    row_x = lax.broadcasted_iota(jnp.int32, (EXTRA, LANES), 0)
    ones = jnp.ones((EXTRA, tokens), jnp.bfloat16)

    def rs_move(k):
        to = lax.rem(c + k, nc)
        return pltpu.make_async_remote_copy(
            src_ref=part.at[to], dst_ref=rs.at[k],
            send_sem=rs_send.at[k], recv_sem=rs_recv.at[k],
            device_id=(b, to), device_id_type=MESH,
        )

    k_copy.wait()
    v_copy.wait()

    def partials(k, carry):
        to = lax.rem(c + k, nc)
        for i in range(ppd):
            at = pl.multiple_of((i * nc + to) * LANES, LANES)
            feature = softplus(kt[pl.ds(at, LANES), :])
            left = jnp.concatenate([vt[pl.ds(at, LANES), :], ones], axis=0)
            s = lax.dot_general(left, feature, (((1,), (1,)), ((), ())), preferred_element_type=jnp.float32)
            part[to, i, :size, :] = jnp.where(lane, s[:size], s[size : 2 * size]).astype(jnp.bfloat16)
            part[to, i, size:, :] = split_mass(s[2 * size :])

        @pl.when(k > 1)
        def _():
            rs_move(k - 1).start()

        return carry

    lax.fori_loop(1, nc + 1, partials, 0)

    for k in range(1, nc):
        rs_move(k).wait_recv()
    for i in range(ppd):
        s = part[c, i].astype(jnp.float32)
        for k in range(1, nc):
            s = s + rs[k, i].astype(jnp.float32)
        s = s / count
        own[i, :size, :] = s[:size].astype(jnp.bfloat16)
        m = jnp.broadcast_to(s[size : size + 1] + s[size + 1 : size + 2], (EXTRA, LANES))
        own[i, size:, :] = split_mass(m)

    def ag_move(i, k):
        p = i * nc + c
        g, slot = p // ppg, lax.rem(p, ppg)
        to = lax.rem(c + k, nc)
        landing = b * ppg + slot
        remote = pltpu.make_async_remote_copy(
            src_ref=own.at[i], dst_ref=st.at[landing],
            send_sem=ag_send.at[i * nc + k], recv_sem=ag_recv.at[landing],
            device_id=(g, to), device_id_type=MESH,
        )
        local = pltpu.make_async_copy(own.at[i], st.at[landing], ag_recv.at[landing])
        return g, remote, local

    for k in range(nc):
        for i in range(ppd):
            g, remote, local = ag_move(i, k)
            if k > 0:
                remote.start()
            else:
                pl.when(g != b)(remote.start)
                pl.when(g == b)(local.start)

    for k in range(nb):
        if k == 0:
            q_copy.wait()
        else:
            q_move(nb - k).wait_recv()

        def featured(i, carry):
            at = pl.multiple_of(i * LANES, LANES)
            qx[k, pl.ds(at, LANES), :] = softplus(qx[k, pl.ds(at, LANES), :])
            return carry

        lax.fori_loop(0, ppg, featured, 0)

    for k in range(nb):
        s = lax.rem(b + k, nb)
        for slot in range(ppg):
            at = s * ppg + slot
            pltpu.make_async_copy(st.at[at], st.at[at], ag_recv.at[at]).wait()
            state = st[at, :size, :]
            mass = st[at, size:, :].astype(jnp.float32)
            hi, lo = mass[0:1], mass[1:2]
            low_half = jnp.where(lane_x, jnp.where(row_x == 0, hi, lo), 0.0)
            high_half = jnp.where(lane_x, 0.0, jnp.where(row_x == 2, hi, lo))
            m = jnp.where(row_x < 2, low_half, jnp.where(row_x < 4, high_half, 0.0)).astype(jnp.bfloat16)
            zero = jnp.zeros_like(state)
            left = jnp.concatenate([jnp.where(lane, state, zero), jnp.where(lane, zero, state), m], axis=0)
            both = lax.dot_general(
                left, qx[k, slot * LANES : (slot + 1) * LANES, :], (((1,), (0,)), ((), ())),
                preferred_element_type=jnp.float32,
            )
            low = both[2 * size :]
            first = count**0.5 / (low[0:1] + low[1:2] + 0.001)
            second = count**0.5 / (low[2:3] + low[3:4] + 0.001)
            read = jnp.concatenate([both[:size] * first, both[size : 2 * size] * second], axis=0)
            mixed[k * tokens : (k + 1) * tokens, slot * LANES : (slot + 1) * LANES] = read.T.astype(jnp.bfloat16)

    def pr_move(j, k):
        return pltpu.make_async_remote_copy(
            src_ref=out_buf.at[j, k - 1], dst_ref=in_buf.at[j, k - 1],
            send_sem=pr_send.at[j, k - 1], recv_sem=pr_recv.at[j, k - 1],
            device_id=(lax.rem(b + k, nb), c), device_id_type=MESH,
        )

    w_copy.wait()
    width = o_ref.shape[1] // chunks

    def project(j, carry):
        at = pl.multiple_of(j * width, width)
        y = jnp.dot(mixed[...], wv[:, pl.ds(at, width)], preferred_element_type=jnp.float32)
        for k in range(1, nb):
            out_buf[j, k - 1] = y[k * tokens : (k + 1) * tokens].astype(jnp.bfloat16)
        mine[:, pl.ds(at, width)] = y[:tokens]
        for k in range(1, nb):
            pr_move(j, k).start()
        return carry

    lax.fori_loop(0, chunks, project, 0)

    def collect(j, carry):
        at = pl.multiple_of(j * width, width)
        y = mine[:, pl.ds(at, width)]
        for k in range(1, nb):
            pr_move(j, k).wait_recv()
            y = y + in_buf[j, k - 1].astype(jnp.float32)
        o_ref[:, pl.ds(at, width)] = y.astype(jnp.bfloat16)
        return carry

    lax.fori_loop(0, chunks, collect, 0)

    for k in range(1, nb):
        q_move(k).wait_send()

    def rs_end(k, carry):
        rs_move(k).wait_send()
        return carry

    lax.fori_loop(1, nc, rs_end, 0)
    for k in range(nc):
        for i in range(ppd):
            g, remote, local = ag_move(i, k)
            if k > 0:
                remote.wait_send()
            else:
                pl.when(g != b)(remote.wait_send)

    def pr_end(j, carry):
        for k in range(1, nb):
            pr_move(j, k).wait_send()
        return carry

    lax.fori_loop(0, chunks, pr_end, 0)


def solution(mesh):
    nb, nc = mesh.shape["batch"], mesh.shape["ctx"]

    def shards(asked_for, offered, contents, out_weight):
        _, tokens, heads, size = asked_for.shape
        rows = heads * size
        depth, columns = out_weight.shape
        pairs = rows // LANES
        block = size + EXTRA
        width = CHUNK if columns % CHUNK == 0 else columns
        chunks = columns // width

        def flat(x):
            return x.transpose(0, 2, 3, 1).reshape(rows, tokens)

        bf16, f32 = jnp.bfloat16, jnp.float32
        dma = pltpu.SemaphoreType.DMA
        out = pl.pallas_call(
            functools.partial(kernel, nb, nc, size),
            out_shape=jax.ShapeDtypeStruct((tokens, columns), bf16),
            in_specs=[pl.BlockSpec(memory_space=pl.ANY)] * 4,
            out_specs=pl.BlockSpec(memory_space=pltpu.VMEM),
            scratch_shapes=[
                pltpu.VMEM((rows, tokens), bf16),
                pltpu.VMEM((rows, tokens), bf16),
                pltpu.VMEM((depth, columns), bf16),
                pltpu.VMEM((nb, rows // nb, tokens), bf16),
                pltpu.VMEM((nc, pairs // nc, block, LANES), bf16),
                pltpu.VMEM((nc, pairs // nc, block, LANES), bf16),
                pltpu.VMEM((pairs // nc, block, LANES), bf16),
                pltpu.VMEM((pairs, block, LANES), bf16),
                pltpu.VMEM((nb * tokens, rows // nb), bf16),
                pltpu.VMEM((chunks, nb - 1, tokens, width), bf16),
                pltpu.VMEM((tokens, columns), f32),
                pltpu.VMEM((chunks, nb - 1, tokens, width), bf16),
                dma((4,)),
                dma((nb,)),
                dma((nb,)),
                dma((nc,)),
                dma((nc,)),
                dma((pairs,)),
                dma((pairs,)),
                dma((chunks, nb - 1)),
                dma((chunks, nb - 1)),
            ],
            compiler_params=pltpu.CompilerParams(
                collective_id=0, has_side_effects=True, vmem_limit_bytes=60 * 2**20
            ),
        )(flat(asked_for), flat(offered), flat(contents), out_weight)
        return out[None]

    in_specs = (
        P("batch", "ctx", None, None),
        P("batch", "ctx", None, None),
        P("batch", "ctx", None, None),
        P("batch", None),
    )
    return jax.shard_map(
        shards, mesh=mesh, in_specs=in_specs, out_specs=P("batch", "ctx", None), check_vma=False
    )
```

time: 331 us -> 94.9 us (0.29)
  waiting for transfers between devices: 163 us -> 0 us
  Pallas kernels: 0 us -> 91.6 us
  blocking collectives: 81.2 us -> 0 us
  local copies, waits for them, and re-layouts: 29.2 us -> 2.29 us
  matrix products: 17.8 us -> 0 us
  between operations: 13.5 us -> 0.01 us
  other arithmetic: 12.3 us -> 0 us
  starting transfers between devices: 11.3 us -> 0 us
    all_gather x1 -> x0, waiting for transfers between devices: 123 us -> none  [shards(): lax.all_gather(out_weight, 'batch', axis=0, tiled=True)]
    pallas_call x0 -> x1, Pallas kernels: none -> 91.6 us  [shards(): pl.pallas_call(functools.partial(kernel, nb, nc, size), out_shape=jax.Sha...]
    all_to_all x2 -> x0, blocking collectives: 81.2 us -> none  [the longest x1 52.2 us: shards(): lax.all_to_all(head_read, 'ctx', split_axis=1, concat_axis=2, tiled=True)]
    all_to_all x2 -> x0, waiting for transfers between devices: 39.6 us -> none  [the longest x1 22.8 us: shards(): lax.all_to_all(query_feature, 'ctx', split_axis=2, concat_axis=1, tiled=T...]
    dot_general x3 -> x0, matrix products: 17.8 us -> none  [the longest x1 14 us: shards(): jnp.einsum('btw,wv->btv', mixed, lax.all_gather(out_weight, 'batch', axis...]
    all_to_all x2 -> x0, starting transfers between devices: 11.3 us -> none  [the longest x1 6.04 us: shards(): lax.all_to_all(contents, 'ctx', split_axis=2, concat_axis=1, tiled=True)]
    all_to_all x5 -> x0, local copies, waits for them, and re-layouts: 8.42 us -> none  [the longest x2 3.34 us: shards(): lax.all_to_all(head_read, 'ctx', split_axis=1, concat_axis=2, tiled=True)]
    unnamed x9 -> x1, local copies, waits for them, and re-layouts: 10.4 us -> 2.29 us
  transfers between devices with their start and end apart: 3 -> 0, of which waited for: 3 -> 0; matrix products, arithmetic and copies ran while one was open for 14% -> 0% of each run, Pallas kernels for 0% -> 0%
where the time goes in v1:
time: 94.9 us; the launch traced here: 93.8 us
  Pallas kernels  91.6 us (97%)
  local copies, waits for them, and re-layouts  2.29 us (2%)
    pallas_call x1, Pallas kernels, shards(): pl.pallas_call(functools.partial(kernel, nb, nc, size), out_shape=jax.Sha...  91.6 us
    unnamed x1, local copies, waits for them, and re-layouts  2.29 us

profile of v1, /device:TPU:24, one launch (start us, length us, event | category | flops | bytes accessed | tf_op | source)
XLA Modules:
  0.0 93.8 jit_solution(16716493203345756913)
XLA Ops:
  0.0 91.6 %shard_map.46 = bf16[128,4096]{1,0:T(8,128)(2,1)} custom-call(bf16[4096,128]{1,0:T(8,128)(2,1)} %bitcast.11, bf16[4096,128]{1,0:T(8,128)(2,1)} %bitcast.12, bf16[4096,128]{1,0:T(8,128)(2,1)} %bitcast.13, bf16[1024,4096]{1,0:T(8,128)(2,1)} %w_ref.1), custom_call_target="tpu_custom_call" | custom-call | tf_op jit(solution)/shard_map/pallas_call | solution.py:248
  91.6 2.3 %copy.6 = bf16[1,128,4096]{2,1,0:T(8,128)(2,1)} copy(bf16[1,128,4096]{2,1,0:T(8,128)(2,1)} %bitcast.10) | data formatting | bytes 2097152

commit v2 on v1

--- a/solution.py
+++ b/solution.py
@@ -1,4 +1,5 @@
 import functools
+import math
 
 import jax
 import jax.numpy as jnp
@@ -25,11 +26,12 @@
 
 
 def kernel(
-    nb, nc, size, q_ref, k_ref, v_ref, w_ref, o_ref,
-    kt, vt, wv, qx, part, rs, own, st, mixed, out_buf, mine, in_buf,
-    local_sem, q_send, q_recv, rs_send, rs_recv, ag_send, ag_recv, pr_send, pr_recv,
+    ny, nx, nc, size, q_ref, k_ref, v_ref, w_ref, o_ref,
+    kt, vt, wv, qx, part, rs, own, st, mixed, mine, stage1, stage2,
+    local_sem, q_send, q_recv, rs_send, rs_recv, ag_send, ag_recv,
 ):
     b, c = lax.axis_index("batch"), lax.axis_index("ctx")
+    nb = ny * nx
     rows, tokens = k_ref.shape
     pairs = rows // LANES
     ppg, ppd = pairs // nb, pairs // nc
@@ -37,7 +39,7 @@
     total = nb * nc
     me = b * nc + c
     count = tokens * nc
-    chunks = out_buf.shape[0]
+    chunks = mine[0].shape[0]
 
     barrier = pltpu.get_barrier_semaphore()
 
@@ -57,11 +59,19 @@
     w_copy.start()
     pl.semaphore_wait(barrier, total - 1)
 
+    y_me, x_me = b // nx, lax.rem(b, nx)
+
+    def ahead(k):
+        return lax.rem(y_me + k // nx, ny) * nx + lax.rem(x_me + k % nx, nx)
+
+    def back(k):
+        return (ny - k // nx) % ny * nx + (nx - k % nx) % nx
+
     def q_move(k):
-        to = lax.rem(b + k, nb)
+        to = ahead(k)
         return pltpu.make_async_remote_copy(
-            src_ref=q_ref.at[pl.ds(to * group, group)], dst_ref=qx.at[nb - k],
-            send_sem=q_send.at[k], recv_sem=q_recv.at[nb - k],
+            src_ref=q_ref.at[pl.ds(to * group, group)], dst_ref=qx.at[back(k)],
+            send_sem=q_send.at[k], recv_sem=q_recv.at[back(k)],
             device_id=(to, c), device_id_type=MESH,
         )
 
@@ -139,7 +149,7 @@
         if k == 0:
             q_copy.wait()
         else:
-            q_move(nb - k).wait_recv()
+            q_move(back(k)).wait_recv()
 
         def featured(i, carry):
             at = pl.multiple_of(i * LANES, LANES)
@@ -149,7 +159,7 @@
         lax.fori_loop(0, ppg, featured, 0)
 
     for k in range(nb):
-        s = lax.rem(b + k, nb)
+        s = ahead(k)
         for slot in range(ppg):
             at = s * ppg + slot
             pltpu.make_async_copy(st.at[at], st.at[at], ag_recv.at[at]).wait()
@@ -171,35 +181,85 @@
             read = jnp.concatenate([both[:size] * first, both[size : 2 * size] * second], axis=0)
             mixed[k * tokens : (k + 1) * tokens, slot * LANES : (slot + 1) * LANES] = read.T.astype(jnp.bfloat16)
 
-    def pr_move(j, k):
+    w_copy.wait()
+
+    width = o_ref.shape[1] // chunks
+    half = width // 2
+
+    def place(axis, k):
+        if axis == 0:
+            return (y_me * nx + lax.rem(x_me + k, nx), c)
+        return (lax.rem(y_me + k, ny) * nx + x_me, c)
+
+    def offset(axis, k, other):
+        return (other * nx + k) if axis == 0 else (k * nx + other)
+
+    def first_move(j, h, k):
+        n2 = ny if h == 0 else nx
+        at = pl.ds((k - 1) * n2, n2)
+        out_buf, in_buf, send, recv = stage1[h]
+        return pltpu.make_async_remote_copy(
+            src_ref=out_buf.at[j, at], dst_ref=in_buf.at[j, at],
+            send_sem=send.at[j, k - 1], recv_sem=recv.at[j, k - 1],
+            device_id=place(h, k), device_id_type=MESH,
+        )
+
+    def second_move(j, h, k):
+        out_buf, in_buf, send, recv = stage2[h]
         return pltpu.make_async_remote_copy(
             src_ref=out_buf.at[j, k - 1], dst_ref=in_buf.at[j, k - 1],
-            send_sem=pr_send.at[j, k - 1], recv_sem=pr_recv.at[j, k - 1],
-            device_id=(lax.rem(b + k, nb), c), device_id_type=MESH,
-        )
-
-    w_copy.wait()
-    width = o_ref.shape[1] // chunks
+            send_sem=send.at[j, k - 1], recv_sem=recv.at[j, k - 1],
+            device_id=place(1 - h, k), device_id_type=MESH,
+        )
+
+    sizes = ((nx, ny), (ny, nx))
 
     def project(j, carry):
         at = pl.multiple_of(j * width, width)
         y = jnp.dot(mixed[...], wv[:, pl.ds(at, width)], preferred_element_type=jnp.float32)
-        for k in range(1, nb):
-            out_buf[j, k - 1] = y[k * tokens : (k + 1) * tokens].astype(jnp.bfloat16)
-        mine[:, pl.ds(at, width)] = y[:tokens]
-        for k in range(1, nb):
-            pr_move(j, k).start()
+        for h, (n1, n2) in enumerate(sizes):
+            for k in range(n1):
+                for other in range(n2):
+                    r = offset(h, k, other) * tokens
+                    piece = y[r : r + tokens, h * half : (h + 1) * half]
+                    if k > 0:
+                        stage1[h][0][j, (k - 1) * n2 + other] = piece.astype(jnp.bfloat16)
+                    else:
+                        mine[h][j, other] = piece
+        for h, (n1, n2) in enumerate(sizes):
+            for k in range(1, n1):
+                first_move(j, h, k).start()
         return carry
 
     lax.fori_loop(0, chunks, project, 0)
 
+    def relay(j, carry):
+        for h, (n1, n2) in enumerate(sizes):
+            for k in range(1, n1):
+                first_move(j, h, k).wait_recv()
+            for other in range(n2):
+                y = mine[h][j, other]
+                for k in range(1, n1):
+                    y = y + stage1[h][1][j, (k - 1) * n2 + other].astype(jnp.float32)
+                if other > 0:
+                    stage2[h][0][j, other - 1] = y.astype(jnp.bfloat16)
+                else:
+                    mine[h][j, 0] = y
+        for h, (n1, n2) in enumerate(sizes):
+            for k in range(1, n2):
+                second_move(j, h, k).start()
+        return carry
+
+    lax.fori_loop(0, chunks, relay, 0)
+
     def collect(j, carry):
-        at = pl.multiple_of(j * width, width)
-        y = mine[:, pl.ds(at, width)]
-        for k in range(1, nb):
-            pr_move(j, k).wait_recv()
-            y = y + in_buf[j, k - 1].astype(jnp.float32)
-        o_ref[:, pl.ds(at, width)] = y.astype(jnp.bfloat16)
+        for h, (n1, n2) in enumerate(sizes):
+            at = pl.multiple_of(j * width + h * half, half)
+            y = mine[h][j, 0]
+            for k in range(1, n2):
+                second_move(j, h, k).wait_recv()
+                y = y + stage2[h][1][j, k - 1].astype(jnp.float32)
+            o_ref[:, pl.ds(at, half)] = y.astype(jnp.bfloat16)
         return carry
 
     lax.fori_loop(0, chunks, collect, 0)
@@ -221,8 +281,11 @@
                 pl.when(g != b)(remote.wait_send)
 
     def pr_end(j, carry):
-        for k in range(1, nb):
-            pr_move(j, k).wait_send()
+        for h, (n1, n2) in enumerate(sizes):
+            for k in range(1, n1):
+                first_move(j, h, k).wait_send()
+            for k in range(1, n2):
+                second_move(j, h, k).wait_send()
         return carry
 
     lax.fori_loop(0, chunks, pr_end, 0)
@@ -230,6 +293,8 @@
 
 def solution(mesh):
     nb, nc = mesh.shape["batch"], mesh.shape["ctx"]
+    nx = next(n for n in range(math.isqrt(nb), 0, -1) if nb % n == 0)
+    ny = nb // nx
 
     def shards(asked_for, offered, contents, out_weight):
         _, tokens, heads, size = asked_for.shape
@@ -245,8 +310,14 @@
 
         bf16, f32 = jnp.bfloat16, jnp.float32
         dma = pltpu.SemaphoreType.DMA
+        sizes = ((nx, ny), (ny, nx))
+
+        def stage(blocks, moves):
+            buffer = pltpu.VMEM((chunks, blocks, tokens, width // 2), bf16)
+            return [buffer, buffer, dma((chunks, moves)), dma((chunks, moves))]
+
         out = pl.pallas_call(
-            functools.partial(kernel, nb, nc, size),
+            functools.partial(kernel, ny, nx, nc, size),
             out_shape=jax.ShapeDtypeStruct((tokens, columns), bf16),
             in_specs=[pl.BlockSpec(memory_space=pl.ANY)] * 4,
             out_specs=pl.BlockSpec(memory_space=pltpu.VMEM),
@@ -260,9 +331,9 @@
                 pltpu.VMEM((pairs // nc, block, LANES), bf16),
                 pltpu.VMEM((pairs, block, LANES), bf16),
                 pltpu.VMEM((nb * tokens, rows // nb), bf16),
-                pltpu.VMEM((chunks, nb - 1, tokens, width), bf16),
-                pltpu.VMEM((tokens, columns), f32),
-                pltpu.VMEM((chunks, nb - 1, tokens, width), bf16),
+                [pltpu.VMEM((chunks, n2, tokens, width // 2), f32) for _, n2 in sizes],
+                [stage((n1 - 1) * n2, n1 - 1) for n1, n2 in sizes],
+                [stage(n2 - 1, n2 - 1) for _, n2 in sizes],
                 dma((4,)),
                 dma((nb,)),
                 dma((nb,)),
@@ -270,8 +341,6 @@
                 dma((nc,)),
                 dma((pairs,)),
                 dma((pairs,)),
-                dma((chunks, nb - 1)),
-                dma((chunks, nb - 1)),
             ],
             compiler_params=pltpu.CompilerParams(
                 collective_id=0, has_side_effects=True, vmem_limit_bytes=60 * 2**20

time: 94.9 us -> 83.5 us (0.88)
  Pallas kernels: 91.6 us -> 80.3 us
    pallas_call x1, Pallas kernels: 91.6 us -> 80.3 us  [shards(): pl.pallas_call(functools.partial(kernel, ny, nx, nc, size), out_shape=jax...]
where the time goes in v2:
time: 83.5 us; the launch traced here: 82.6 us
  Pallas kernels  80.3 us (96%)
  local copies, waits for them, and re-layouts  2.29 us (3%)
    pallas_call x1, Pallas kernels, shards(): pl.pallas_call(functools.partial(kernel, ny, nx, nc, size), out_shape=jax...  80.3 us
    unnamed x1, local copies, waits for them, and re-layouts  2.29 us

profile of v2, /device:TPU:24, one launch (start us, length us, event | category | flops | bytes accessed | tf_op | source)
XLA Modules:
  0.0 82.6 jit_solution(12350875517531149250)
XLA Ops:
  0.0 80.3 %shard_map.46 = bf16[128,4096]{1,0:T(8,128)(2,1)} custom-call(bf16[4096,128]{1,0:T(8,128)(2,1)} %bitcast.11, bf16[4096,128]{1,0:T(8,128)(2,1)} %bitcast.12, bf16[4096,128]{1,0:T(8,128)(2,1)} %bitcast.13, bf16[1024,4096]{1,0:T(8,128)(2,1)} %w_ref.1), custom_call_target="tpu_custom_call" | custom-call | tf_op jit(solution)/shard_map/pallas_call | solution.py:319
  80.3 2.3 %copy.6 = bf16[1,128,4096]{2,1,0:T(8,128)(2,1)} copy(bf16[1,128,4096]{2,1,0:T(8,128)(2,1)} %bitcast.10) | data formatting | bytes 2097152

commit v3 on v2

--- a/solution.py
+++ b/solution.py
@@ -27,8 +27,9 @@
 
 def kernel(
     ny, nx, nc, size, q_ref, k_ref, v_ref, w_ref, o_ref,
-    kt, vt, wv, qx, part, rs, own, st, mixed, mine, stage1, stage2,
-    local_sem, q_send, q_recv, rs_send, rs_recv, ag_send, ag_recv,
+    kt, vt, wv, qx, part, part_in, both, rs, own, st, mixed, mine, stage1, stage2,
+    local_sem, q_send, q_recv, pa_send, pa_recv, rs_send, rs_recv,
+    ag_send, ag_recv, fw_send, fw_recv,
 ):
     b, c = lax.axis_index("batch"), lax.axis_index("ctx")
     nb = ny * nx
@@ -83,26 +84,60 @@
     row_x = lax.broadcasted_iota(jnp.int32, (EXTRA, LANES), 0)
     ones = jnp.ones((EXTRA, tokens), jnp.bfloat16)
 
+    nz, z_me, odd = nc // 2, c // 2, lax.rem(c, 2)
+    partner = z_me * 2 + 1 - odd
+
+    def pa_move(k):
+        return pltpu.make_async_remote_copy(
+            src_ref=part.at[k - 1], dst_ref=part_in.at[k - 1],
+            send_sem=pa_send.at[k - 1], recv_sem=pa_recv.at[k - 1],
+            device_id=(b, partner), device_id_type=MESH,
+        )
+
     def rs_move(k):
-        to = lax.rem(c + k, nc)
-        return pltpu.make_async_remote_copy(
-            src_ref=part.at[to], dst_ref=rs.at[k],
-            send_sem=rs_send.at[k], recv_sem=rs_recv.at[k],
-            device_id=(b, to), device_id_type=MESH,
-        )
+        return pltpu.make_async_remote_copy(
+            src_ref=both.at[k - 1], dst_ref=rs.at[k - 1],
+            send_sem=rs_send.at[k - 1], recv_sem=rs_recv.at[k - 1],
+            device_id=(b, lax.rem(z_me + k, nz) * 2 + odd), device_id_type=MESH,
+        )
+
+    def partial_sum(i, to):
+        at = pl.multiple_of((i * nc + to) * LANES, LANES)
+        feature = softplus(kt[pl.ds(at, LANES), :])
+        left = jnp.concatenate([vt[pl.ds(at, LANES), :], ones], axis=0)
+        s = lax.dot_general(left, feature, (((1,), (1,)), ((), ())), preferred_element_type=jnp.float32)
+        return jnp.where(lane, s[:size], s[size : 2 * size]), s[2 * size :]
+
+    def mass_of(block):
+        return block[size : size + 1].astype(jnp.float32) + block[size + 1 : size + 2].astype(jnp.float32)
 
     k_copy.wait()
     v_copy.wait()
 
-    def partials(k, carry):
-        to = lax.rem(c + k, nc)
+    def for_partner(k, carry):
+        to = lax.rem(z_me + k, nz) * 2 + 1 - odd
         for i in range(ppd):
-            at = pl.multiple_of((i * nc + to) * LANES, LANES)
-            feature = softplus(kt[pl.ds(at, LANES), :])
-            left = jnp.concatenate([vt[pl.ds(at, LANES), :], ones], axis=0)
-            s = lax.dot_general(left, feature, (((1,), (1,)), ((), ())), preferred_element_type=jnp.float32)
-            part[to, i, :size, :] = jnp.where(lane, s[:size], s[size : 2 * size]).astype(jnp.bfloat16)
-            part[to, i, size:, :] = split_mass(s[2 * size :])
+            state, mass = partial_sum(i, to)
+            part[k - 1, i, :size, :] = state.astype(jnp.bfloat16)
+            part[k - 1, i, size:, :] = split_mass(mass)
+
+        @pl.when(k > 1)
+        def _():
+            pa_move(k - 1).start()
+
+        return carry
+
+    lax.fori_loop(1, nz + 1, for_partner, 0)
+    pa_move(nz).start()
+
+    def for_chip(k, carry):
+        to = lax.rem(z_me + k, nz) * 2 + odd
+        sums = [partial_sum(i, to) for i in range(ppd)]
+        pa_move(k).wait_recv()
+        for i, (state, mass) in enumerate(sums):
+            block = part_in[k - 1, i]
+            both[k - 1, i, :size, :] = (state + block[:size].astype(jnp.float32)).astype(jnp.bfloat16)
+            both[k - 1, i, size:, :] = split_mass(mass + mass_of(block))
 
         @pl.when(k > 1)
         def _():
@@ -110,33 +145,39 @@
 
         return carry
 
-    lax.fori_loop(1, nc + 1, partials, 0)
-
-    for k in range(1, nc):
+    lax.fori_loop(1, nz + 1, for_chip, 0)
+
+    for k in range(1, nz):
         rs_move(k).wait_recv()
     for i in range(ppd):
-        s = part[c, i].astype(jnp.float32)
-        for k in range(1, nc):
-            s = s + rs[k, i].astype(jnp.float32)
-        s = s / count
-        own[i, :size, :] = s[:size].astype(jnp.bfloat16)
-        m = jnp.broadcast_to(s[size : size + 1] + s[size + 1 : size + 2], (EXTRA, LANES))
-        own[i, size:, :] = split_mass(m)
+        blocks = [both[nz - 1, i]] + [rs[k - 1, i] for k in range(1, nz)]
+        state = sum(x[:size].astype(jnp.float32) for x in blocks) / count
+        mass = sum(mass_of(x) for x in blocks) / count
+        own[i, :size, :] = state.astype(jnp.bfloat16)
+        own[i, size:, :] = split_mass(jnp.broadcast_to(mass, (EXTRA, LANES)))
 
     def ag_move(i, k):
         p = i * nc + c
         g, slot = p // ppg, lax.rem(p, ppg)
-        to = lax.rem(c + k, nc)
+        to = lax.rem(z_me + k, nz) * 2 + odd
         landing = b * ppg + slot
         remote = pltpu.make_async_remote_copy(
             src_ref=own.at[i], dst_ref=st.at[landing],
-            send_sem=ag_send.at[i * nc + k], recv_sem=ag_recv.at[landing],
+            send_sem=ag_send.at[i * nz + k], recv_sem=ag_recv.at[landing],
             device_id=(g, to), device_id_type=MESH,
         )
         local = pltpu.make_async_copy(own.at[i], st.at[landing], ag_recv.at[landing])
         return g, remote, local
 
-    for k in range(nc):
+    def fw_move(k, u):
+        landing = ahead(k) * ppg + 2 * u + odd
+        return pltpu.make_async_remote_copy(
+            src_ref=st.at[landing], dst_ref=st.at[landing],
+            send_sem=fw_send.at[landing], recv_sem=fw_recv.at[landing],
+            device_id=(b, partner), device_id_type=MESH,
+        )
+
+    for k in range(nz):
         for i in range(ppd):
             g, remote, local = ag_move(i, k)
             if k > 0:
@@ -158,28 +199,38 @@
 
         lax.fori_loop(0, ppg, featured, 0)
 
+    def read(k, slot):
+        at = ahead(k) * ppg + slot
+        state = st[at, :size, :]
+        mass = st[at, size:, :].astype(jnp.float32)
+        hi, lo = mass[0:1], mass[1:2]
+        low_half = jnp.where(lane_x, jnp.where(row_x == 0, hi, lo), 0.0)
+        high_half = jnp.where(lane_x, 0.0, jnp.where(row_x == 2, hi, lo))
+        m = jnp.where(row_x < 2, low_half, jnp.where(row_x < 4, high_half, 0.0)).astype(jnp.bfloat16)
+        zero = jnp.zeros_like(state)
+        left = jnp.concatenate([jnp.where(lane, state, zero), jnp.where(lane, zero, state), m], axis=0)
+        column = pl.multiple_of(slot * LANES, LANES)
+        y = lax.dot_general(
+            left, qx[k, pl.ds(column, LANES), :], (((1,), (0,)), ((), ())),
+            preferred_element_type=jnp.float32,
+        )
+        low = y[2 * size :]
+        first = count**0.5 / (low[0:1] + low[1:2] + 0.001)
+        second = count**0.5 / (low[2:3] + low[3:4] + 0.001)
+        y = jnp.concatenate([y[:size] * first, y[size : 2 * size] * second], axis=0)
+        mixed[k * tokens : (k + 1) * tokens, pl.ds(column, LANES)] = y.T.astype(jnp.bfloat16)
+
     for k in range(nb):
-        s = ahead(k)
-        for slot in range(ppg):
-            at = s * ppg + slot
+        for u in range(ppg // 2):
+            at = ahead(k) * ppg + 2 * u + odd
             pltpu.make_async_copy(st.at[at], st.at[at], ag_recv.at[at]).wait()
-            state = st[at, :size, :]
-            mass = st[at, size:, :].astype(jnp.float32)
-            hi, lo = mass[0:1], mass[1:2]
-            low_half = jnp.where(lane_x, jnp.where(row_x == 0, hi, lo), 0.0)
-            high_half = jnp.where(lane_x, 0.0, jnp.where(row_x == 2, hi, lo))
-            m = jnp.where(row_x < 2, low_half, jnp.where(row_x < 4, high_half, 0.0)).astype(jnp.bfloat16)
-            zero = jnp.zeros_like(state)
-            left = jnp.concatenate([jnp.where(lane, state, zero), jnp.where(lane, zero, state), m], axis=0)
-            both = lax.dot_general(
-                left, qx[k, slot * LANES : (slot + 1) * LANES, :], (((1,), (0,)), ((), ())),
-                preferred_element_type=jnp.float32,
-            )
-            low = both[2 * size :]
-            first = count**0.5 / (low[0:1] + low[1:2] + 0.001)
-            second = count**0.5 / (low[2:3] + low[3:4] + 0.001)
-            read = jnp.concatenate([both[:size] * first, both[size : 2 * size] * second], axis=0)
-            mixed[k * tokens : (k + 1) * tokens, slot * LANES : (slot + 1) * LANES] = read.T.astype(jnp.bfloat16)
+            fw_move(k, u).start()
+            read(k, 2 * u + odd)
+    for k in range(nb):
+        for u in range(ppg // 2):
+            at = ahead(k) * ppg + 2 * u + 1 - odd
+            pltpu.make_async_copy(st.at[at], st.at[at], fw_recv.at[at]).wait()
+            read(k, 2 * u + 1 - odd)
 
     w_copy.wait()
 
@@ -267,18 +318,20 @@
     for k in range(1, nb):
         q_move(k).wait_send()
 
-    def rs_end(k, carry):
+    for k in range(1, nz + 1):
+        pa_move(k).wait_send()
+    for k in range(1, nz):
         rs_move(k).wait_send()
-        return carry
-
-    lax.fori_loop(1, nc, rs_end, 0)
-    for k in range(nc):
+    for k in range(nz):
         for i in range(ppd):
             g, remote, local = ag_move(i, k)
             if k > 0:
                 remote.wait_send()
             else:
                 pl.when(g != b)(remote.wait_send)
+    for k in range(nb):
+        for u in range(ppg // 2):
+            fw_move(k, u).wait_send()
 
     def pr_end(j, carry):
         for h, (n1, n2) in enumerate(sizes):
@@ -326,8 +379,10 @@
                 pltpu.VMEM((rows, tokens), bf16),
                 pltpu.VMEM((depth, columns), bf16),
                 pltpu.VMEM((nb, rows // nb, tokens), bf16),
-                pltpu.VMEM((nc, pairs // nc, block, LANES), bf16),
-                pltpu.VMEM((nc, pairs // nc, block, LANES), bf16),
+                pltpu.VMEM((nc // 2, pairs // nc, block, LANES), bf16),
+                pltpu.VMEM((nc // 2, pairs // nc, block, LANES), bf16),
+                pltpu.VMEM((nc // 2, pairs // nc, block, LANES), bf16),
+                pltpu.VMEM((nc // 2, pairs // nc, block, LANES), bf16),
                 pltpu.VMEM((pairs // nc, block, LANES), bf16),
                 pltpu.VMEM((pairs, block, LANES), bf16),
                 pltpu.VMEM((nb * tokens, rows // nb), bf16),
@@ -337,8 +392,12 @@
                 dma((4,)),
                 dma((nb,)),
                 dma((nb,)),
-                dma((nc,)),
-                dma((nc,)),
+                dma((nc // 2,)),
+                dma((nc // 2,)),
+                dma((nc // 2,)),
+                dma((nc // 2,)),
+                dma((pairs // 2,)),
+                dma((pairs,)),
                 dma((pairs,)),
                 dma((pairs,)),
             ],

time: 83.5 us -> 72.9 us (0.87)
  Pallas kernels: 80.3 us -> 70.5 us
    pallas_call x1, Pallas kernels: 80.3 us -> 70.5 us  [shards(): pl.pallas_call(functools.partial(kernel, ny, nx, nc, size), out_shape=jax...]
where the time goes in v3:
time: 72.9 us; the launch traced here: 72.7 us
  Pallas kernels  70.5 us (97%)
  local copies, waits for them, and re-layouts  2.29 us (3%)
    pallas_call x1, Pallas kernels, shards(): pl.pallas_call(functools.partial(kernel, ny, nx, nc, size), out_shape=jax...  70.5 us
    unnamed x1, local copies, waits for them, and re-layouts  2.29 us

profile of v3, /device:TPU:24, one launch (start us, length us, event | category | flops | bytes accessed | tf_op | source)
XLA Modules:
  0.0 72.7 jit_solution(11110134602747093631)
XLA Ops:
  0.0 70.5 %shard_map.46 = bf16[128,4096]{1,0:T(8,128)(2,1)} custom-call(bf16[4096,128]{1,0:T(8,128)(2,1)} %bitcast.11, bf16[4096,128]{1,0:T(8,128)(2,1)} %bitcast.12, bf16[4096,128]{1,0:T(8,128)(2,1)} %bitcast.13, bf16[1024,4096]{1,0:T(8,128)(2,1)} %w_ref.1), custom_call_target="tpu_custom_call" | custom-call | tf_op jit(solution)/shard_map/pallas_call | solution.py:372
  70.5 2.3 %copy.6 = bf16[1,128,4096]{2,1,0:T(8,128)(2,1)} copy(bf16[1,128,4096]{2,1,0:T(8,128)(2,1)} %bitcast.10) | data formatting | bytes 2097152

commit v4 on v3

--- a/solution.py
+++ b/solution.py
@@ -11,7 +11,7 @@
 MESH = pl.DeviceIdType.MESH
 LANES = 128
 EXTRA = 16
-CHUNK = 512
+CHUNK = 256
 
 
 def softplus(x):
@@ -114,23 +114,17 @@
     k_copy.wait()
     v_copy.wait()
 
-    def for_partner(k, carry):
+    for k in range(1, nz + 1):
         to = lax.rem(z_me + k, nz) * 2 + 1 - odd
         for i in range(ppd):
             state, mass = partial_sum(i, to)
             part[k - 1, i, :size, :] = state.astype(jnp.bfloat16)
             part[k - 1, i, size:, :] = split_mass(mass)
-
-        @pl.when(k > 1)
-        def _():
+        if k > 1:
             pa_move(k - 1).start()
-
-        return carry
-
-    lax.fori_loop(1, nz + 1, for_partner, 0)
     pa_move(nz).start()
 
-    def for_chip(k, carry):
+    for k in range(1, nz + 1):
         to = lax.rem(z_me + k, nz) * 2 + odd
         sums = [partial_sum(i, to) for i in range(ppd)]
         pa_move(k).wait_recv()
@@ -138,14 +132,8 @@
             block = part_in[k - 1, i]
             both[k - 1, i, :size, :] = (state + block[:size].astype(jnp.float32)).astype(jnp.bfloat16)
             both[k - 1, i, size:, :] = split_mass(mass + mass_of(block))
-
-        @pl.when(k > 1)
-        def _():
+        if k > 1:
             rs_move(k - 1).start()
-
-        return carry
-
-    lax.fori_loop(1, nz + 1, for_chip, 0)
 
     for k in range(1, nz):
         rs_move(k).wait_recv()

time: 72.9 us -> 73.4 us (level)
  no operation moved by 1% of the time
where the time goes in v4:
time: 73.4 us; the launch traced here: 72.9 us
  Pallas kernels  70.6 us (96%)
  local copies, waits for them, and re-layouts  2.29 us (3%)
    pallas_call x1, Pallas kernels, shards(): pl.pallas_call(functools.partial(kernel, ny, nx, nc, size), out_shape=jax...  70.6 us
    unnamed x1, local copies, waits for them, and re-layouts  2.29 us

profile of v4, /device:TPU:24, one launch (start us, length us, event | category | flops | bytes accessed | tf_op | source)
XLA Modules:
  0.0 72.9 jit_solution(13793647942424573123)
XLA Ops:
  0.0 70.6 %shard_map.46 = bf16[128,4096]{1,0:T(8,128)(2,1)} custom-call(bf16[4096,128]{1,0:T(8,128)(2,1)} %bitcast.11, bf16[4096,128]{1,0:T(8,128)(2,1)} %bitcast.12, bf16[4096,128]{1,0:T(8,128)(2,1)} %bitcast.13, bf16[1024,4096]{1,0:T(8,128)(2,1)} %w_ref.1), custom_call_target="tpu_custom_call" | custom-call | tf_op jit(solution)/shard_map/pallas_call | solution.py:360
  70.6 2.3 %copy.6 = bf16[1,128,4096]{2,1,0:T(8,128)(2,1)} copy(bf16[1,128,4096]{2,1,0:T(8,128)(2,1)} %bitcast.10) | data formatting | bytes 2097152
